TPU v7x, 256 devices: a whole 4x4x8 slice. The times are simulated.
256 devices in a mesh: tok: 16 (over z, core), vocab: 16 (over y, x).
Axes of the slice: x: 4, y: 4, z: 8, core: 2. Of those that a mesh axis runs over, the one named last changes fastest.
Arguments:
- latent_vectors: float32 [1536, 3584], P('tok'), may hold values from -400 to 400
- unembedding_matrix: float32 [3584, 152064], P(None, ('tok', 'vocab')), may hold values from -0.09375 to 0.09375
- drawn_symbols: int32 [1536], P('tok'), may hold values from 0 to 152063
- piece_extents: int32 [16, 4], P('tok'), may hold values from 1 to 48, 96 in all within a row
- piece_episode_lookup: int32 [16, 4], P('tok'), may hold values from 0 to 1023
- episode_heats: float32 [1024], replicated, may hold values from 0.6 to 1.5
Outputs:
- seg_logprob: float32 [64], P('tok')
Inputs may be any that keep to these rules, and one draw needn't show every extreme that they name: `piece_extents`: each row of lengths sums to 96.
All inputs are finite; a program needn't handle non-finite values.
Results may differ from a plain program's by a relative error of at most 0.0003.
Values sent between devices are 32-bit elements; how exact they have to be, the bound alone decides.
A program may use at most 128 MiB of HBM per device.

v0:
```python
import jax
import jax.numpy as jnp
from jax import lax
from jax.sharding import Mesh
from jax.sharding import PartitionSpec as P

TOK = ("tok_0", "tok_1")
VOCAB = ("vocab_0", "vocab_1")
TOK_VOCAB = ("tok_0", "tok_1", "vocab_0", "vocab_1")


def collected_together(x, axis):
    leaves = jax.tree.leaves(x)
    order = sorted(range(len(leaves)), key=lambda k: -leaves[k].size)
    width = (1, *leaves[order[0]].shape)[-1]
    lines = [
        jnp.pad(leaves[k].reshape(-1), (0, -leaves[k].size % width)).reshape(-1, width)
        for k in order
    ]
    both, at, found = (lax.all_gather(jnp.concatenate(lines), axis), 0, {})
    for k, line in zip(order, lines):
        piece = both[:, at : at + len(line)].reshape(len(both), -1)
        found[k] = piece[:, : leaves[k].size].reshape(-1, *leaves[k].shape)
        at += len(line)
    numbers = iter(range(len(leaves)))
    return jax.tree.map(lambda _: found[next(numbers)], x)


def merged_by_axis(x, axes, combine):
    for axis in axes:
        pieces = collected_together(x, axis)
        x = jax.tree.map(lambda part: part[0], pieces)
        for k in range(1, lax.axis_size(axis)):
            x = combine(x, jax.tree.map(lambda part: part[k], pieces))
    return x


def combine_pairs(earlier, later):
    peak = jnp.maximum(earlier[0], later[0])
    total = earlier[1] * jnp.exp(earlier[0] - peak) + later[1] * jnp.exp(later[0] - peak)
    return (peak, total, earlier[2] + later[2])


def on_device(
    latent_vectors,
    unembedding_matrix,
    drawn_symbols,
    piece_extents,
    piece_episode_lookup,
    episode_heats,
):
    tok_rows = latent_vectors.shape[0]
    ends = jnp.cumsum(piece_extents[0])
    starts = ends - piece_extents[0]
    position = jnp.arange(tok_rows, dtype=jnp.int32)
    piece_episode = (
        (position[None, :] >= starts[:, None]) & (position[None, :] < ends[:, None])
    ).astype(jnp.float32)
    chosen_symbol = (
        piece_episode_lookup[0][:, None]
        == jnp.arange(episode_heats.shape[0], dtype=jnp.int32)[None, :]
    ).astype(jnp.float32)
    piece_reciprocal_heat = jnp.dot(
        chosen_symbol, 1.0 / episode_heats, precision=lax.Precision.HIGHEST
    )
    symbol_reciprocal_heat = jnp.dot(
        piece_reciprocal_heat, piece_episode, precision=lax.Precision.HIGHEST
    )
    gathered, scale_all, target_all = (
        lax.all_gather(latent_vectors, TOK, axis=0, tiled=True),
        lax.all_gather(symbol_reciprocal_heat, TOK, axis=0, tiled=True),
        lax.all_gather(drawn_symbols, TOK, axis=0, tiled=True),
    )
    width = unembedding_matrix.shape[1]
    column_start = (lax.axis_index(TOK) * lax.axis_size(VOCAB) + lax.axis_index(VOCAB)) * width
    logits = (
        jnp.dot(
            gathered,
            unembedding_matrix,
            preferred_element_type=jnp.float32,
            precision=lax.Precision.HIGHEST,
        )
        * scale_all[:, None]
    )
    ids = column_start + jnp.arange(width, dtype=jnp.int32)
    picked = jnp.sum(jnp.where(target_all[:, None] == ids[None, :], logits, 0.0), axis=1)
    local_top = jnp.max(logits, axis=1)
    local_total = jnp.sum(jnp.exp(logits - local_top[:, None]), axis=1)
    top, total, target_logit = merged_by_axis(
        (local_top, local_total, picked), TOK_VOCAB, combine_pairs
    )
    logprob = target_logit - top - jnp.log(total)
    own = lax.dynamic_slice_in_dim(logprob, lax.axis_index(TOK) * tok_rows, tok_rows, 0)
    sums = jnp.dot(piece_episode, own, precision=lax.Precision.HIGHEST)
    return sums / piece_extents[0].astype(jnp.float32)


def solution(mesh):
    finer = Mesh(mesh.devices.reshape(8, 2, 4, 4), ("tok_0", "tok_1", "vocab_0", "vocab_1"))
    return jax.shard_map(
        on_device,
        mesh=finer,
        in_specs=(P(TOK, None), P(None, TOK_VOCAB), P(TOK), P(TOK, None), P(TOK, None), P()),
        out_specs=P(TOK),
        check_vma=False,
    )
```

profile of v0, /device:TPU:2, one launch (start us, length us, event | category | flops | bytes accessed | tf_op | source)
XLA Modules:
  0.0 244.3 jit_solution(13467237366138529779)
XLA Ops:
  6.5 0.0 all-gather.10.cloned.1.call-start
  6.5 0.7 all-gather.10.cloned.1.call-update
  7.3 0.8 reduce-window.7
  8.1 1.3 dynamic-slice
  10.0 0.7 bitcast_subtract_fusion
  10.7 0.7 broadcast_divide_fusion
  11.4 0.8 convolution_bitcast_fusion.2
  12.2 0.2 convolution_bitcast_fusion.1
  12.4 0.2 dynamic-update-slice
  12.6 0.8 dynamic-update-slice.1
  13.5 32.3 %all-reduce = f32[1536]{0:T(1024)S(1)} all-reduce(f32[1536]{0:T(1024)S(1)} %dynamic-update-slice), channel_id=1, replica_groups=mesh['tok_0'=8,'tok_1'=2,'vocab_0'=4,'vocab_1'=4] {'tok_0','tok_1'}, use_global_device_ids=true, to_apply=%add | all-reduce | flops 1536 | bytes 12288
  45.8 10.6 %all-reduce.1 = s32[1536]{0:T(1024)S(1)} all-reduce(s32[1536]{0:T(1024)S(1)} %dynamic-update-slice.1), channel_id=1, replica_groups=mesh['tok_0'=8,'tok_1'=2,'vocab_0'=4,'vocab_1'=4] {'tok_0','tok_1'}, use_global_device_ids=true, to_apply=%add.1 | all-reduce | flops 1536 | bytes 12288
  56.3 76.7 %all-gather.10.cloned.1.call-done = f32[1536,3584]{1,0:T(8,128)} async-done(((f32[96,3584]{1,0:T(8,128)}), f32[1536,3584]{1,0:T(8,128)}) %all-gather.10.cloned.1.call-update) | async-done | bytes 22020112 | tf_op jit(solution)/shard_map/all_gather | solution.py:70
  133.1 51.2 %fusion.65 = (f32[1536]{0:T(1024)S(1)}, f32[1536,594]{0,1:T(8,128)S(1)}) fusion(f32[1536]{0:T(1024)S(1)} %all-reduce, f32[1536,3584]{1,0:T(8,128)} %all-gather.10.cloned.1.call-done, f32[3584,594]{0,1:T(8,128)} %param.7), kind=kOutput, calls=%fused_computation.134 | convolution fusion | flops 39241633792 | bytes 34197504 | tf_op jit(solution)/shard_map/dot_general | solution.py:77
  184.3 0.0 copy-start
  184.3 0.9 exponential_reduce_fusion
  185.2 24.7 %all-gather.4 = f32[8,3,1536]{2,1,0:T(4,128)S(1)} all-gather(f32[1,3,1536]{2,1,0:T(4,128)S(1)} %maximum_bitcast_fusion), channel_id=2, replica_groups=mesh['tok_0'=8,'tok_1'=2,'vocab_0'=4,'vocab_1'=4] {'tok_0'}, dimensions={0}, use_global_device_ids=true | all-gather | bytes 165888 | tf_op jit(solution)/shard_map/all_gather | solution.py:20
  210.0 0.1 fusion.19
  210.2 1.8 all-gather.5
  212.1 12.3 %all-gather.6 = f32[4,3,1536]{2,1,0:T(4,128)S(1)} all-gather(f32[1,3,1536]{2,1,0:T(4,128)S(1)} %maximum_bitcast_fusion.2), channel_id=4, replica_groups=mesh['tok_0'=8,'tok_1'=2,'vocab_0'=4,'vocab_1'=4] {'vocab_0'}, dimensions={0}, use_global_device_ids=true | all-gather | bytes 92160 | tf_op jit(solution)/shard_map/all_gather | solution.py:20
  224.4 0.1 fusion.5
  224.5 11.9 %all-gather.7 = f32[4,3,1536]{2,1,0:T(4,128)S(1)} all-gather(f32[1,3,1536]{2,1,0:T(4,128)S(1)} %maximum_bitcast_fusion.3), channel_id=5, replica_groups=mesh['tok_0'=8,'tok_1'=2,'vocab_0'=4,'vocab_1'=4] {'vocab_1'}, dimensions={0}, use_global_device_ids=true | all-gather | bytes 92160 | tf_op jit(solution)/shard_map/all_gather | solution.py:20
  236.4 0.2 slice_reduce_fusion.3
  236.7 0.0 copy-done
  236.7 0.7 fusion
  (17 shorter events, 0.3 us)
Async XLA Ops:
  6.5 126.5 %all-gather.10.cloned.1.call-start = ((), (), s32[]{:S(2)}) async-start(), calls=%async_computation | async-start | bytes 23396352 | tf_op jit(solution)/shard_map/all_gather | solution.py:70
  184.3 52.4 %copy-start = (s32[1,4]{1,0:T(1,128)S(1)}, s32[1,4]{1,0:T(1,128)}, u32[]{:S(2)}) copy-start(s32[1,4]{1,0:T(1,128)} %param.9) | copy-start | bytes 52
Sparse Core Ops, SparseCore 0:
  9.2 123.8 all-gather.9
where the time goes:
time: 244 us
  blocking collectives  93.6 us (38%)
  waiting for transfers between devices  77.4 us (32%)
  matrix products  53 us (22%)
  between operations  14.2 us (6%)
  other arithmetic  3.67 us (2%)
    all_gather x1, waiting for transfers between devices, on_device(): lax.all_gather(latent_vectors, TOK, axis=0, tiled=True)  76.7 us
    dot_general x1, matrix products, on_device(): jnp.dot(gathered, unembedding_matrix, preferred_element_type=jnp.float32,...  51.2 us
    all_gather x4, blocking collectives, collected_together(): both, at, found = (lax.all_gather(jnp.concatenate(lines), axis), 0, {})  50.7 us
    unnamed x2, blocking collectives  42.8 us
  transfers between devices with their start and end apart: 1, of which 1 were waited for; matrix products, arithmetic and copies ran while one was open for 2% of the time, Pallas kernels for 0%

commit v1 on v0

--- a/solution.py
+++ b/solution.py
@@ -67,7 +67,12 @@
         piece_reciprocal_heat, piece_episode, precision=lax.Precision.HIGHEST
     )
     gathered, scale_all, target_all = (
-        lax.all_gather(latent_vectors, TOK, axis=0, tiled=True),
+        jnp.concatenate(
+            lax.all_to_all(
+                jnp.stack([latent_vectors for _ in range(lax.psum(1, TOK))], axis=0), TOK, 0, 0
+            ),
+            0,
+        ),
         lax.all_gather(symbol_reciprocal_heat, TOK, axis=0, tiled=True),
         lax.all_gather(drawn_symbols, TOK, axis=0, tiled=True),
     )

time: 244 us -> 634 us (2.60)
  blocking collectives: 93.6 us -> 557 us
  waiting for transfers between devices: 77.4 us -> 0.01 us
  between operations: 14.2 us -> 0.88 us
  local copies, waits for them, and re-layouts: 2.34 us -> 12.6 us
  starting transfers between devices: 0.01 us -> 8.76 us
    unnamed x2, blocking collectives: 42.8 us -> 505 us
    all_gather x1 -> x0, waiting for transfers between devices: 76.7 us -> none  [on_device(): lax.all_gather(latent_vectors, TOK, axis=0, tiled=True)]
    another operation x0 -> x1, local copies, waits for them, and re-layouts: none -> 11.5 us  [on_device(): jnp.stack([latent_vectors for _ in range(lax.psum(1, TOK))], axis=0)]
    all_to_all x0 -> x1, starting transfers between devices: none -> 8.76 us  [on_device(): lax.all_to_all(jnp.stack([latent_vectors for _ in range(lax.psum(1, TOK))...]
  transfers between devices with their start and end apart: 1 -> 1, of which waited for: 1 -> 0; matrix products, arithmetic and copies ran while one was open for 2% -> 0% of each run, Pallas kernels for 0% -> 0%
where the time goes in v1:
time: 634 us; the launch traced here: 633 us
  blocking collectives  557 us (88%)
  matrix products  52.4 us (8%)
  local copies, waits for them, and re-layouts  12.6 us (2%)
  starting transfers between devices  8.76 us (1%)
    unnamed x2, blocking collectives  505 us
    all_gather x4, blocking collectives, collected_together(): both, at, found = (lax.all_gather(jnp.concatenate(lines), axis), 0, {})  52 us
    dot_general x1, matrix products, on_device(): jnp.dot(gathered, unembedding_matrix, preferred_element_type=jnp.float32,...  51.2 us
  transfers between devices with their start and end apart: 1, of which 0 were waited for; matrix products, arithmetic and copies ran while one was open for 0% of the time, Pallas kernels for 0%

profile of v1, /device:TPU:2, one launch (start us, length us, event | category | flops | bytes accessed | tf_op | source)
XLA Modules:
  0.0 633.4 jit_solution(15765267473105432334)
XLA Ops:
  0.0 11.5 %stack.2 = f32[16,96,3584]{2,1,0:T(8,128)} broadcast(f32[96,3584]{1,0:T(8,128)} %param.6), dimensions={1,2} | broadcast | bytes 23396352 | tf_op jit(solution)/shard_map/stack | solution.py:72
  11.5 0.0 copy-start.3
  11.5 0.0 copy-start.4
  11.5 0.0 copy-start
  11.5 0.0 copy-start.1
  11.5 0.0 copy-start.2
  11.5 8.8 %all-to-all-start = ((f32[16,96,3584]{2,1,0:T(8,128)}), f32[16,96,3584]{2,1,0:T(8,128)}, u32[]{:S(2)}, u32[]{:S(2)}) async-start(f32[16,96,3584]{2,1,0:T(8,128)} %stack.2), calls=%async_computation | async-start | bytes 44040192 | tf_op jit(solution)/shard_map/all_to_all | solution.py:71
  20.3 0.0 copy-done.3
  20.3 0.2 reduce-window.7
  20.5 0.0 copy-done.4
  20.5 0.6 dynamic-slice
  21.8 0.0 copy-done
  21.8 0.0 copy-done.1
  21.8 0.2 convolution_bitcast_fusion.2
  22.0 0.2 convolution_bitcast_fusion.1
  22.2 0.2 dynamic-update-slice
  22.4 0.0 copy-done.2
  22.4 0.3 dynamic-update-slice.1
  22.7 493.0 %all-reduce = f32[1536]{0:T(1024)S(1)} all-reduce(f32[1536]{0:T(1024)S(1)} %dynamic-update-slice), channel_id=1, replica_groups=mesh['tok_0'=8,'tok_1'=2,'vocab_0'=4,'vocab_1'=4] {'tok_0','tok_1'}, use_global_device_ids=true, to_apply=%add | all-reduce | flops 1536 | bytes 12288
  515.7 12.1 %all-reduce.1 = s32[1536]{0:T(1024)S(1)} all-reduce(s32[1536]{0:T(1024)S(1)} %dynamic-update-slice.1), channel_id=1, replica_groups=mesh['tok_0'=8,'tok_1'=2,'vocab_0'=4,'vocab_1'=4] {'tok_0','tok_1'}, use_global_device_ids=true, to_apply=%add.1 | all-reduce | flops 1536 | bytes 12288
  527.8 0.0 all-to-all-done
  527.8 51.2 %fusion.65 = (f32[1536]{0:T(1024)S(1)}, f32[1536,594]{0,1:T(8,128)S(1)}) fusion(f32[1536]{0:T(1024)S(1)} %all-reduce, f32[1536,3584]{1,0:T(8,128)} %bitcast.3, f32[3584,594]{0,1:T(8,128)} %param.7), kind=kOutput, calls=%fused_computation.134 | convolution fusion | flops 39241633792 | bytes 34197504 | tf_op jit(solution)/shard_map/dot_general | solution.py:82
  579.1 0.9 exponential_reduce_fusion
  580.0 25.7 %all-gather.4 = f32[8,3,1536]{2,1,0:T(4,128)S(1)} all-gather(f32[1,3,1536]{2,1,0:T(4,128)S(1)} %maximum_bitcast_fusion), channel_id=2, replica_groups=mesh['tok_0'=8,'tok_1'=2,'vocab_0'=4,'vocab_1'=4] {'tok_0'}, dimensions={0}, use_global_device_ids=true | all-gather | bytes 165888 | tf_op jit(solution)/shard_map/all_gather | solution.py:20
  605.8 0.1 fusion.19
  605.9 1.8 all-gather.5
  607.9 12.4 %all-gather.6 = f32[4,3,1536]{2,1,0:T(4,128)S(1)} all-gather(f32[1,3,1536]{2,1,0:T(4,128)S(1)} %maximum_bitcast_fusion.2), channel_id=4, replica_groups=mesh['tok_0'=8,'tok_1'=2,'vocab_0'=4,'vocab_1'=4] {'vocab_0'}, dimensions={0}, use_global_device_ids=true | all-gather | bytes 92160 | tf_op jit(solution)/shard_map/all_gather | solution.py:20
  620.3 0.1 fusion.5
  620.4 12.0 %all-gather.7 = f32[4,3,1536]{2,1,0:T(4,128)S(1)} all-gather(f32[1,3,1536]{2,1,0:T(4,128)S(1)} %maximum_bitcast_fusion.3), channel_id=5, replica_groups=mesh['tok_0'=8,'tok_1'=2,'vocab_0'=4,'vocab_1'=4] {'vocab_1'}, dimensions={0}, use_global_device_ids=true | all-gather | bytes 92160 | tf_op jit(solution)/shard_map/all_gather | solution.py:20
  632.4 0.2 slice_reduce_fusion.3
  632.6 0.7 fusion
  (19 shorter events, 0.3 us)
Async XLA Ops:
  11.5 8.8 %copy-start.3 = (s32[1,4]{1,0:T(1,128)S(1)}, s32[1,4]{1,0:T(1,128)}, u32[]{:S(2)}) copy-start(s32[1,4]{1,0:T(1,128)} %param.9) | copy-start | bytes 52
  11.5 9.0 %copy-start.4 = (u32[256]{0:T(256)S(1)}, u32[256]{0:T(256)}, u32[]{:S(2)}) copy-start(u32[256]{0:T(256)} %constant.47) | copy-start | bytes 3076
  11.5 10.2 %copy-start = (f32[1024]{0:T(1024)S(1)}, f32[1024]{0:T(1024)}, u32[]{:S(2)}) copy-start(f32[1024]{0:T(1024)} %param.11) | copy-start | bytes 12292
  11.5 10.3 %copy-start.1 = (s32[1,4]{1,0:T(1,128)S(1)}, s32[1,4]{1,0:T(1,128)}, u32[]{:S(2)}) copy-start(s32[1,4]{1,0:T(1,128)} %param.10) | copy-start | bytes 52
  11.5 10.9 %copy-start.2 = (s32[96]{0:T(128)S(1)}, s32[96]{0:T(128)}, u32[]{:S(2)}) copy-start(s32[96]{0:T(128)} %param.8) | copy-start | bytes 1156
  11.5 516.3 %all-to-all-start = ((f32[16,96,3584]{2,1,0:T(8,128)}), f32[16,96,3584]{2,1,0:T(8,128)}, u32[]{:S(2)}, u32[]{:S(2)}) async-start(f32[16,96,3584]{2,1,0:T(8,128)} %stack.2), calls=%async_computation | async-start | bytes 44040192 | tf_op jit(solution)/shard_map/all_to_all | solution.py:71
